TPU v7x, 512 devices: a whole 4x8x8 slice. The times are simulated.
512 devices in a mesh: probe: 4 (over x), seq: 128 (over y, z, core).
Axes of the slice: x: 4, y: 8, z: 8, core: 2. Of those that a mesh axis runs over, the one named last changes fastest.
Arguments:
- probe_bits: int32 [4, 128, 16384], P('probe', 'seq'), may hold values from 0 to 1
- noise_var: float32 [128, 16384], P('seq'), may hold values from 0.2 to 12
- kernel_spectrum: float32 [16384, 128], P('seq'), may hold values from 0.05 to 4, as said below
- symbol: float32 [16384, 128], P('seq'), may hold values from 0.3 to 3, as said below
- grad_prev: float32 [16384, 128], P('seq', 'probe'), may hold values from -6 to 6
Outputs:
- residual: float32 [4, 128, 16384], P('probe', 'seq')
- grad_total: float32 [16384, 128], P('seq', 'probe')
Inputs may be any that keep to these rules, and one draw needn't show every extreme that they name: kernel_spectrum at frequency k equals kernel_spectrum at frequency (2097152 - k) mod 2097152. symbol at frequency k equals symbol at frequency (2097152 - k) mod 2097152.
All inputs are finite; a program needn't handle non-finite values.
Results may differ from a plain program's by a relative error of at most 0.00017.
Values sent between devices are 32-bit elements; how exact they have to be, the bound alone decides.
A program may use at most 64 MiB of HBM per device.

v0:
```python
import math

import jax
import jax.numpy as jnp
from jax import lax
from jax.sharding import PartitionSpec as P

highest = lax.Precision.HIGHEST
minor_width = 128


def dft_table(height, breadth, modulus, orient):
    left_index = jnp.arange(height, dtype=jnp.int32)[:, None]
    right_index = jnp.arange(breadth, dtype=jnp.int32)[None, :]
    phases = (
        orient * 2.0 * math.pi / modulus * (left_index * right_index % modulus).astype(jnp.float32)
    )
    return (jnp.cos(phases), jnp.sin(phases))


def complex_product(pattern, real_part, imaginary, cosine_table, sine_table):
    real_cos = jnp.einsum(pattern, real_part, cosine_table, precision=highest)
    real_sin = jnp.einsum(pattern, real_part, sine_table, precision=highest)
    if imaginary is None:
        return (real_cos, real_sin)
    imag_cos = jnp.einsum(pattern, imaginary, cosine_table, precision=highest)
    imag_sin = jnp.einsum(pattern, imaginary, sine_table, precision=highest)
    return (real_cos - imag_sin, real_sin + imag_cos)


def rotate(real_part, imaginary, cosine_table, sine_table):
    return (
        real_part * cosine_table - imaginary * sine_table,
        real_part * sine_table + imaginary * cosine_table,
    )


def forward_rows(series):
    major_len = series.shape[-2]
    length = major_len * minor_width
    cosine_table, sine_table = dft_table(major_len, major_len, major_len, -1.0)
    section_real, section_imag = complex_product(
        "...mi,mk->...ik", series, None, cosine_table, sine_table
    )
    turn_cos, turn_sin = dft_table(minor_width, major_len, length, -1.0)
    twisted_real, twisted_imag = rotate(section_real, section_imag, turn_cos, turn_sin)
    cosine_table, sine_table = dft_table(minor_width, minor_width, minor_width, -1.0)
    return complex_product("...ik,ij->...jk", twisted_real, twisted_imag, cosine_table, sine_table)


def inverse_rows(real_part, imaginary):
    major_len = real_part.shape[-1]
    length = major_len * minor_width
    cosine_table, sine_table = dft_table(minor_width, minor_width, minor_width, 1.0)
    section_real, section_imag = complex_product(
        "...jk,ji->...ik", real_part, imaginary, cosine_table, sine_table
    )
    turn_cos, turn_sin = dft_table(minor_width, major_len, length, 1.0)
    twisted_real, twisted_imag = rotate(section_real, section_imag, turn_cos, turn_sin)
    cosine_table, sine_table = dft_table(major_len, major_len, major_len, 1.0)
    final_real, unused = complex_product(
        "...ik,km->...mi", twisted_real, twisted_imag, cosine_table, sine_table
    )
    return final_real


def global_twiddle(local_rows, major_len, samples, orient):
    row_index = lax.axis_index("seq") * local_rows + jnp.arange(local_rows, dtype=jnp.int32)
    column_index = (
        jnp.arange(minor_width, dtype=jnp.int32)[:, None] * major_len
        + jnp.arange(major_len, dtype=jnp.int32)[None, :]
    )
    phases = (
        orient
        * 2.0
        * math.pi
        / samples
        * (row_index[:, None, None] * column_index[None, :, :] % samples).astype(jnp.float32)
    )
    return (jnp.cos(phases), jnp.sin(phases))


def forward_spectrum(series):
    local_rows = series.shape[1]
    major_len = series.shape[2]
    devices = lax.axis_size("seq")
    all_rows = local_rows * devices
    samples = all_rows * major_len * minor_width
    real_part, imaginary = forward_rows(series)
    turn_cos, turn_sin = global_twiddle(local_rows, major_len, samples, -1.0)
    turned_real, turned_imag = rotate(real_part, imaginary, turn_cos, turn_sin)
    arrived = lax.all_to_all(
        jnp.stack([turned_real, turned_imag]), "seq", split_axis=3, concat_axis=2, tiled=True
    )
    block = minor_width // devices * major_len
    arrived = arrived.reshape(arrived.shape[0], arrived.shape[1], all_rows, block)
    cosine_table, sine_table = dft_table(all_rows, all_rows, all_rows, -1.0)
    return complex_product("zrb,ra->zba", arrived[0], arrived[1], cosine_table, sine_table)


def inverse_field(spectrum_real, spectrum_imag):
    all_rows = spectrum_real.shape[2]
    block = spectrum_real.shape[1]
    devices = lax.axis_size("seq")
    major_len = block * devices // minor_width
    cosine_table, sine_table = dft_table(all_rows, all_rows, all_rows, 1.0)
    back_real, back_imag = complex_product(
        "zba,ar->zrb", spectrum_real, spectrum_imag, cosine_table, sine_table
    )
    stacked = jnp.stack([back_real, back_imag])
    stacked = stacked.reshape(
        stacked.shape[0], stacked.shape[1], all_rows, minor_width // devices, major_len
    )
    arrived = lax.all_to_all(stacked, "seq", split_axis=2, concat_axis=3, tiled=True)
    local_rows = arrived.shape[2]
    samples = all_rows * major_len * minor_width
    turn_cos, turn_sin = global_twiddle(local_rows, major_len, samples, 1.0)
    turned_real, turned_imag = rotate(arrived[0], arrived[1], turn_cos, turn_sin)
    return inverse_rows(turned_real, turned_imag) / samples


def shards(probe_bits, noise_var, kernel_spectrum, symbol, grad_prev):
    field_shape = (
        probe_bits.shape[0],
        probe_bits.shape[1],
        probe_bits.shape[2] // minor_width,
        minor_width,
    )
    sign_field = (2 * probe_bits - 1).astype(jnp.float32).reshape(field_shape)
    noise_field = noise_var.reshape(field_shape[1:])
    samples = kernel_spectrum.shape[1] * noise_var.shape[1]
    base_real, base_imag = forward_spectrum(sign_field)
    scaled_real = base_real / symbol
    scaled_imag = base_imag / symbol
    precond = inverse_field(scaled_real, scaled_imag)
    again_real, again_imag = forward_spectrum(precond)
    circulant = inverse_field(kernel_spectrum * again_real, kernel_spectrum * again_imag)
    kernel_image = circulant + noise_field * precond
    numerator, curvature = lax.psum(
        (jnp.sum(sign_field * precond), jnp.sum(precond * kernel_image)), "seq"
    )
    step_size = numerator / curvature
    residual = sign_field - step_size * kernel_image
    cross_term = lax.psum(jnp.sum(residual * kernel_image), "seq")
    weight = -2.0 * cross_term
    resid_real, resid_imag = forward_spectrum(residual)
    applied = (
        inverse_field(kernel_spectrum * resid_real, kernel_spectrum * resid_imag)
        + noise_field * residual
    )
    adjoint = (
        weight / curvature * sign_field
        - 2.0 * weight * step_size / curvature * kernel_image
        - 2.0 * step_size * applied
    )
    adjoint_real, adjoint_imag = forward_spectrum(adjoint)
    local_grad = -(adjoint_real[0] * base_real[0] + adjoint_imag[0] * base_imag[0]) / (
        samples * symbol * symbol
    )
    probes = lax.axis_size("probe")
    summed = lax.psum(local_grad, "probe")
    share_width = summed.shape[1] // probes
    own_share = lax.dynamic_slice_in_dim(
        summed, lax.axis_index("probe") * share_width, share_width, 1
    )
    grad_total = grad_prev + own_share / probes
    return (residual.reshape(probe_bits.shape), grad_total)


def solution(mesh):
    placed = (
        P("probe", "seq", None),
        P("seq", None),
        P("seq", None),
        P("seq", None),
        P("seq", "probe"),
    )
    return jax.shard_map(
        shards,
        mesh=mesh,
        in_specs=placed,
        out_specs=(P("probe", "seq", None), P("seq", "probe")),
        check_vma=False,
    )
```

profile of v0, /device:TPU:1, one launch (start us, length us, event | category | flops | bytes accessed | tf_op | source)
XLA Modules:
  0.0 740.6 jit_solution(7742233880407343323)
XLA Ops:
  7.2 0.9 add_convert_fusion
  9.0 0.7 fusion.76
  9.7 0.7 fusion.64
  10.5 0.7 convolution_add_fusion.13
  11.2 0.9 subtract_bitcast_fusion.3
  12.2 30.7 %all_to_all.28 = f32[2,1,1,128,128]{4,2,1,0,3:T(1,128)S(1)} all-to-all(f32[2,1,1,128,128]{4,2,1,0,3:T(1,128)S(1)} %copy.13), channel_id=1, replica_groups=mesh['probe'=4,'seq'=128] {'seq'}, dimensions={3} | all-to-all | bytes 262144 | tf_op jit(solution)/shard_map/all_to_all | solution.py:92
  47.5 18.1 %all_to_all.29 = f32[2,1,128,1,128]{4,3,1,0,2:T(1,128)S(1)} all-to-all(f32[2,1,128,1,128]{4,3,1,0,2:T(1,128)S(1)} %copy.14), channel_id=1, replica_groups=mesh['probe'=4,'seq'=128] {'seq'}, dimensions={2} | all-to-all | bytes 262144 | tf_op jit(solution)/shard_map/all_to_all | solution.py:114
  65.7 0.7 fusion.82
  66.5 0.7 fusion.88
  67.2 0.7 convolution_subtract_fusion.13
  67.9 0.7 convolution_add_fusion.10
  68.7 0.8 fusion.43
  69.5 0.8 fusion.16
  71.1 0.7 fusion.61
  71.9 0.7 fusion.73
  72.6 0.7 convolution_add_fusion.9
  73.3 0.9 subtract_bitcast_fusion.2
  74.3 18.1 %all_to_all.30 = f32[2,1,1,128,128]{4,2,1,0,3:T(1,128)S(1)} all-to-all(f32[2,1,1,128,128]{4,2,1,0,3:T(1,128)S(1)} %copy.17), channel_id=1, replica_groups=mesh['probe'=4,'seq'=128] {'seq'}, dimensions={3} | all-to-all | bytes 262144 | tf_op jit(solution)/shard_map/all_to_all | solution.py:92
  97.1 17.8 %all_to_all.31 = f32[2,1,128,1,128]{4,3,1,0,2:T(1,128)S(1)} all-to-all(f32[2,1,128,1,128]{4,3,1,0,2:T(1,128)S(1)} %copy.18), channel_id=1, replica_groups=mesh['probe'=4,'seq'=128] {'seq'}, dimensions={2} | all-to-all | bytes 262144 | tf_op jit(solution)/shard_map/all_to_all | solution.py:114
  115.0 0.7 fusion.80
  115.7 0.7 fusion.86
  116.5 0.7 convolution_subtract_fusion.8
  117.2 0.7 convolution_add_fusion.6
  118.0 0.8 fusion.36
  118.8 1.4 multiply_reduce_fusion.1
  120.2 247.9 %all-reduce = (f32[]{:T(128)}, f32[]{:T(128)}) all-reduce(f32[]{:T(128)} %get-tuple-element.7, f32[]{:T(128)} %get-tuple-element.6), channel_id=1, replica_groups=mesh['probe'=4,'seq'=128] {'seq'}, use_global_device_ids=true, to_apply=%region_1.2 | all-reduce | flops 2 | bytes 16 | tf_op jit(solution)/shard_map/psum | solution.py:139
  371.0 0.7 fusion.58
  371.7 0.7 fusion.70
  372.4 0.7 convolution_add_fusion.5
  373.2 0.9 subtract_bitcast_fusion.1
  374.2 19.3 %all_to_all.32 = f32[2,1,1,128,128]{4,2,1,0,3:T(1,128)S(1)} all-to-all(f32[2,1,1,128,128]{4,2,1,0,3:T(1,128)S(1)} %copy.21), channel_id=1, replica_groups=mesh['probe'=4,'seq'=128] {'seq'}, dimensions={3} | all-to-all | bytes 262144 | tf_op jit(solution)/shard_map/all_to_all | solution.py:92
  397.6 0.8 copy.22
  398.4 5.9 all-to-all-start.5
  404.4 248.2 %psum.30 = f32[]{:T(128)} all-reduce(f32[]{:T(128)} %get-tuple-element.10), channel_id=1, replica_groups=mesh['probe'=4,'seq'=128] {'seq'}, use_global_device_ids=true, to_apply=%region_5.6 | all-reduce | flops 1 | bytes 8 | tf_op jit(solution)/shard_map/psum | solution.py:144
  655.3 0.7 fusion.78
  656.1 0.7 fusion.84
  656.8 0.7 convolution_subtract_fusion.3
  657.6 0.7 convolution_add_fusion.2
  658.3 0.8 fusion.29
  659.1 0.8 fusion.20
  660.8 0.7 fusion.55
  661.5 0.7 fusion.67
  662.2 0.7 convolution_add_fusion.1
  662.9 0.9 subtract_bitcast_fusion
  664.0 23.3 %all_to_all.33 = f32[2,1,1,128,128]{4,2,1,0,3:T(1,128)S(1)} all-to-all(f32[2,1,1,128,128]{4,2,1,0,3:T(1,128)S(1)} %copy.25), channel_id=1, replica_groups=mesh['probe'=4,'seq'=128] {'seq'}, dimensions={3} | all-to-all | bytes 262144 | tf_op jit(solution)/shard_map/all_to_all | solution.py:92
  688.7 1.1 fusion.21
  690.7 41.3 %all-reduce.3.cloned.1.call-done = f32[128,128]{1,0:T(8,128)} async-done(((f32[128,128]{1,0:T(8,128)}), f32[128,128]{1,0:T(8,128)}) %all-reduce.3.cloned.1.call-update) | async-done | bytes 65552 | tf_op jit(solution)/shard_map/psum | solution.py:161
  732.0 0.9 multiply_add_fusion
  (72 shorter events, 21.3 us)
Async XLA Ops:
  43.9 0.8 copy-start.4
  93.0 0.8 copy-start.2
  118.0 0.8 copy-start.3
  370.1 289.0 %copy-start = (f32[128,128]{1,0:T(8,128)}, f32[128,128]{1,0:T(8,128)S(1)}, u32[]{:S(2)}) copy-start(f32[128,128]{1,0:T(8,128)S(1)} %get-tuple-element.11) | copy-start | bytes 196612
  398.4 256.8 %all-to-all-start.5 = ((f32[2,1,128,1,128]{4,3,1,0,2:T(1,128)}), f32[2,1,128,1,128]{4,3,1,0,2:T(1,128)S(1)}, u32[]{:S(2)}, u32[]{:S(2)}) async-start(f32[2,1,128,1,128]{4,3,1,0,2:T(1,128)} %copy.22), calls=%async_computation.5 | async-start | bytes 262144 | tf_op jit(solution)/shard_map/all_to_all | solution.py:114
  404.3 327.6 %all-reduce.3.cloned.1.call-start = ((), (), s32[]{:S(2)}) async-start(), calls=%async_computation.7 | async-start | bytes 131072 | tf_op jit(solution)/shard_map/psum | solution.py:161
  689.8 0.7 copy-start.1
Sparse Core Ops, SparseCore 0:
  690.0 41.9 all-reduce.2
where the time goes:
time: 750 us; the launch traced here: 741 us
  blocking collectives  623 us (83%)
  matrix products  43.9 us (6%)
  waiting for transfers between devices  41.3 us (6%)
  between operations  18.9 us (3%)
    psum x1, blocking collectives, shards(): cross_term = lax.psum(jnp.sum(residual * kernel_image), 'seq')  248 us
    psum x1, blocking collectives, shards(): lax.psum((jnp.sum(sign_field * precond), jnp.sum(precond * kernel_image))...  248 us
    all_to_all x4, blocking collectives, forward_spectrum(): lax.all_to_all(jnp.stack([turned_real, turned_imag]), 'seq', split_axis=3...  91.4 us
    psum x1, waiting for transfers between devices, shards(): summed = lax.psum(local_grad, 'probe')  41.3 us
    all_to_all x2, blocking collectives, inverse_field(): lax.all_to_all(stacked, 'seq', split_axis=2, concat_axis=3, tiled=True)  35.9 us
  transfers between devices with their start and end apart: 2, of which 1 were waited for; matrix products, arithmetic and copies ran while one was open for 0% of the time, Pallas kernels for 0%

commit v1 on v0

v1 whole, which is shorter than its diff:
```python
import math

import jax
import jax.numpy as jnp
import numpy as np
from jax import lax
from jax.experimental import pallas as pl
from jax.experimental.pallas import tpu as pltpu
from jax.sharding import PartitionSpec as P

MESH = pl.DeviceIdType.MESH
n = 128
f32 = jnp.float32
bf16 = jnp.bfloat16


def split_np(table):
    table = table.astype(np.float32)
    high = table.astype(jnp.bfloat16)
    low = (table - high.astype(np.float32)).astype(jnp.bfloat16)
    return high, low


def tables(samples):
    index = np.arange(n)
    product = index[:, None] * index[None, :]
    angle = 2.0 * math.pi * (product % n) / n
    cosine, sine = np.cos(angle), np.sin(angle)
    forward = np.block([[cosine, sine], [-sine, cosine]])
    inverse = np.block([[cosine, -sine], [sine, cosine]])
    turn = 2.0 * math.pi * product / (n * n)
    far = 2.0 * math.pi * product / samples
    f_high, f_low = split_np(forward)
    i_high, i_low = split_np(inverse)
    rest = [np.cos(turn), -np.sin(turn), np.cos(far), -np.sin(far)]
    return [f_high, f_low, i_high, i_low] + [part.astype(np.float32) for part in rest]


def split(x):
    high = x.astype(bf16)
    low = (x - high.astype(f32)).astype(bf16)
    return high, low


def mm(a, b):
    return jnp.dot(a, b, preferred_element_type=f32)


def table_left(t_high, t_low, data):
    high, low = split(data)
    return mm(t_high, high) + (mm(t_high, low) + mm(t_low, high))


def table_right(data, t_high, t_low):
    high, low = split(data)
    return mm(high, t_high) + (mm(low, t_high) + mm(high, t_low))


def total(x):
    return jnp.sum(jnp.sum(x, axis=0, keepdims=True), axis=1, keepdims=True)


def kernel(
    probes,
    bits_ref,
    noise_ref,
    kernel_ref,
    symbol_ref,
    prev_ref,
    fh_ref,
    fl_ref,
    ih_ref,
    il_ref,
    tc_ref,
    ts_ref,
    vc_ref,
    vs_ref,
    resid_ref,
    grad_ref,
    out1,
    in1,
    out2,
    in2,
    out3,
    in3,
    out4,
    in4,
    out5,
    in5,
    send,
    recv,
):
    me = lax.axis_index("seq")
    mine = lax.axis_index("probe")
    samples = n * n * n

    barrier = pltpu.get_barrier_semaphore()

    @pl.loop(1, n)
    def _(i):
        peer = lax.rem(me + i, n)
        pl.semaphore_signal(barrier, inc=1, device_id={"seq": peer}, device_id_type=MESH)

    for i in range(1, probes):
        other = lax.rem(mine + i, probes)
        pl.semaphore_signal(barrier, inc=1, device_id={"probe": other}, device_id_type=MESH)

    def exchange(source, target, slot):
        @pl.loop(1, n)
        def _(i):
            peer = lax.rem(me + i, n)
            pltpu.make_async_remote_copy(
                src_ref=source.at[peer],
                dst_ref=target.at[me],
                send_sem=send.at[slot],
                recv_sem=recv.at[slot],
                device_id={"seq": peer},
                device_id_type=MESH,
            ).start()

        pltpu.make_async_copy(source.at[me], target.at[me], recv.at[slot]).start()

    def arrived(target, slot):
        pltpu.make_async_copy(target, target, recv.at[slot]).wait()

    def sent(source, slot):
        part = source.at[pl.ds(0, n - 1)]
        pltpu.make_async_copy(part, part, send.at[slot]).wait()

    turn_c, turn_s = tc_ref[...], ts_ref[...]
    row_c = jnp.broadcast_to(vc_ref[pl.ds(me, 1), :], (n, n))
    row_s = jnp.broadcast_to(vs_ref[pl.ds(me, 1), :], (n, n))
    col_c = jnp.broadcast_to(tc_ref[pl.ds(me, 1), :], (n, n)).T
    col_s = jnp.broadcast_to(ts_ref[pl.ds(me, 1), :], (n, n)).T
    glob_c = col_c * row_c - col_s * row_s
    glob_s = col_c * row_s + col_s * row_c

    def forward(field):
        high, low = split(field)
        right_h, right_l = ih_ref[0:n, :], il_ref[0:n, :]
        part = mm(high, right_h) + (mm(low, right_h) + mm(high, right_l))
        real, imag = part[:, 0:n], part[:, n:]
        data = jnp.concatenate(
            [real * turn_c - imag * turn_s, real * turn_s + imag * turn_c], axis=0
        )
        full = table_left(fh_ref[...], fl_ref[...], data)
        real, imag = full[0:n], full[n:]
        return real * glob_c - imag * glob_s, real * glob_s + imag * glob_c

    def columns(real, imag):
        full = table_left(fh_ref[...], fl_ref[...], jnp.concatenate([real, imag], axis=0))
        return full[0:n], full[n:]

    sign = (2 * bits_ref[...] - 1).astype(f32).T
    noise = noise_ref[...].T
    base = forward(sign)
    out1[:, 0, :] = base[0]
    out1[:, 1, :] = base[1]
    pl.semaphore_wait(barrier, n - 1 + probes - 1)
    exchange(out1, in1, 0)
    noisy = forward(noise * sign)
    out2[:, 0, :] = noisy[0]
    out2[:, 1, :] = noisy[1]
    exchange(out2, in2, 1)
    eig = kernel_ref[...].T
    inv = 1.0 / symbol_ref[...].T

    arrived(in1, 0)
    s_real, s_imag = columns(in1[:, 0, :], in1[:, 1, :])
    scaled_real, scaled_imag = s_real * inv, s_imag * inv
    pair_real = scaled_real - eig * scaled_imag
    pair_imag = scaled_imag + eig * scaled_real
    back = table_left(ih_ref[...], il_ref[...], jnp.concatenate([pair_real, pair_imag], axis=0))
    out3[:, 0, :] = back[0:n]
    out3[:, 1, :] = back[n:]
    exchange(out3, in3, 2)
    power = s_real * s_real + s_imag * s_imag

    arrived(in3, 2)
    real, imag = in3[:, 0, :], in3[:, 1, :]
    data = jnp.concatenate(
        [real * glob_c + imag * glob_s, imag * glob_c - real * glob_s], axis=0
    )
    full = table_left(ih_ref[...], il_ref[...], data)
    real, imag = full[0:n], full[n:]
    data = jnp.concatenate(
        [real * turn_c + imag * turn_s, imag * turn_c - real * turn_s], axis=1
    )
    spatial = table_right(data, fh_ref[...], fl_ref[...]) * (1.0 / samples)
    precond, circulant = spatial[:, 0:n], spatial[:, n:]
    damped = noise * precond
    image = circulant + damped
    sums = [
        total(sign * precond),
        total(precond * image),
        total(sign * image),
        total(image * image),
    ]
    lane = lax.broadcasted_iota(jnp.int32, (1, n), 1)
    line = jnp.zeros((1, n), f32)
    for place, value in enumerate(sums):
        line = jnp.where(lane == place, value, line)
    first = forward(damped)
    second = forward(noise * image)
    for place, value in enumerate((first[0], first[1], second[0], second[1])):
        out4[:, place, 0, :] = value
    out4[:, 4, 0, :] = jnp.broadcast_to(line, (n, n))
    exchange(out4, in4, 3)

    arrived(in2, 1)
    t_real, t_imag = columns(in2[:, 0, :], in2[:, 1, :])
    t_dot = t_real * s_real + t_imag * s_imag

    arrived(in4, 3)
    lines = jnp.sum(in4[:, 4, 0, :], axis=0, keepdims=True)
    numerator, curvature, straight, squared = [
        jnp.sum(jnp.where(lane == place, lines, 0.0), axis=1, keepdims=True) for place in range(4)
    ]
    step = numerator / curvature
    weight = -2.0 * (straight - step * squared)
    over = weight / curvature
    double = 2.0 * over * step
    y_real, y_imag = columns(in4[:, 0, 0, :], in4[:, 1, 0, :])
    y_dot = y_real * s_real + y_imag * s_imag
    q_real, q_imag = columns(in4[:, 2, 0, :], in4[:, 3, 0, :])
    q_dot = q_real * s_real + q_imag * s_imag
    image_dot = eig * inv * power + y_dot
    applied_dot = eig * (power - step * image_dot) + t_dot - step * q_dot
    adjoint_dot = over * power - double * image_dot - (2.0 * step) * applied_dot
    share = adjoint_dot * (inv * inv) * (-1.0 / (samples * probes))
    width = n // probes
    for place in range(probes):
        out5[place] = share[place * width : (place + 1) * width]

    for i in range(1, probes):
        other = lax.rem(mine + i, probes)
        pltpu.make_async_remote_copy(
            src_ref=out5.at[other],
            dst_ref=in5.at[mine],
            send_sem=send.at[4],
            recv_sem=recv.at[4],
            device_id={"probe": other},
            device_id_type=MESH,
        ).start()
    pltpu.make_async_copy(out5.at[mine], in5.at[mine], recv.at[4]).start()
    resid_ref[...] = (sign - step * image).T
    sent(out1, 0)
    sent(out2, 1)
    sent(out3, 2)
    sent(out4, 3)
    arrived(in5, 4)
    own = in5[0]
    for place in range(1, probes):
        own = own + in5[place]
    grad_ref[...] = prev_ref[...] + own.T
    rest = out5.at[pl.ds(0, probes - 1)]
    pltpu.make_async_copy(rest, rest, send.at[4]).wait()


def shards(probes, probe_bits, noise_var, kernel_spectrum, symbol, grad_prev):
    width = grad_prev.shape[1]
    vmem = pl.BlockSpec(memory_space=pltpu.VMEM)
    constants = tables(n * n * n)
    pair = pltpu.VMEM((n, 2, n), f32)
    quad = pltpu.VMEM((n, 5, 1, n), f32)
    quarter = pltpu.VMEM((probes, n // probes, n), f32)
    resid, grad = pl.pallas_call(
        lambda *refs: kernel(probes, *refs),
        out_shape=(
            jax.ShapeDtypeStruct((n, n), f32),
            jax.ShapeDtypeStruct((n, width), f32),
        ),
        in_specs=[vmem] * (5 + len(constants)),
        out_specs=(vmem, vmem),
        scratch_shapes=[pair, pair, pair, pair, pair, pair, quad, quad, quarter, quarter]
        + [pltpu.SemaphoreType.DMA((5,)), pltpu.SemaphoreType.DMA((5,))],
        compiler_params=pltpu.CompilerParams(
            collective_id=0, has_side_effects=True, vmem_limit_bytes=32 * 1024 * 1024
        ),
        name="adjoint_step",
    )(
        probe_bits.reshape(n, n),
        noise_var.reshape(n, n),
        kernel_spectrum,
        symbol,
        grad_prev,
        *[jnp.asarray(part) for part in constants],
    )
    return resid.reshape(probe_bits.shape), grad


def solution(mesh):
    placed = (
        P("probe", "seq", None),
        P("seq", None),
        P("seq", None),
        P("seq", None),
        P("seq", "probe"),
    )
    probes = mesh.shape["probe"]
    return jax.shard_map(
        lambda *args: shards(probes, *args),
        mesh=mesh,
        in_specs=placed,
        out_specs=(P("probe", "seq", None), P("seq", "probe")),
        check_vma=False,
    )
```

time: 750 us -> 66 us (0.09); the launches traced: 741 us -> 65.4 us
  blocking collectives: 623 us -> 0 us
  Pallas kernels: 0 us -> 53.1 us
  matrix products: 43.9 us -> 0 us
  waiting for transfers between devices: 41.3 us -> 0 us
  between operations: 18.9 us -> 0.67 us
    psum x2 -> x0, blocking collectives: 496 us -> none  [the longest x1 248 us: shards(): cross_term = lax.psum(jnp.sum(residual * kernel_image), 'seq')]
    all_to_all x6 -> x0, blocking collectives: 127 us -> none  [the longest x4 91.4 us: forward_spectrum(): lax.all_to_all(jnp.stack([turned_real, turned_imag]), 'seq', split_axis=3...]
    pallas_call x0 -> x1, Pallas kernels: none -> 53.1 us  [shards(): pl.pallas_call(lambda *refs: kernel(probes, *refs), out_shape=(jax.ShapeD...]
    dot_general x70 -> x0, matrix products: 43.9 us -> none  [the longest x21 12.5 us: complex_product(): real_cos = jnp.einsum(pattern, real_part, cosine_table, precision=highest)]
    psum x1 -> x0, waiting for transfers between devices: 41.3 us -> none  [shards(): summed = lax.psum(local_grad, 'probe')]
    unnamed x12 -> x27, local copies, waits for them, and re-layouts: 2.29 us -> 11.6 us
  transfers between devices with their start and end apart: 2 -> 0, of which waited for: 1 -> 0; matrix products, arithmetic and copies ran while one was open for 0% -> 0% of each run, Pallas kernels for 0% -> 0%
where the time goes in v1:
time: 66 us; the launch traced here: 65.4 us
  Pallas kernels  53.1 us (80%)
  local copies, waits for them, and re-layouts  11.6 us (18%)
  between operations  0.67 us (1%)
    pallas_call x1, Pallas kernels, shards(): pl.pallas_call(lambda *refs: kernel(probes, *refs), out_shape=(jax.ShapeD...  53.1 us
    unnamed x27, local copies, waits for them, and re-layouts  11.6 us

profile of v1, /device:TPU:1, one launch (start us, length us, event | category | flops | bytes accessed | tf_op | source)
XLA Modules:
  0.0 65.4 jit_solution(12753633482887111570)
XLA Ops:
  0.6 0.0 copy-start.4
  0.6 0.8 %copy.15.refs_4_ = f32[128,32]{1,0:T(8,128)S(1)} copy(f32[128,32]{0,1:T(8,128)} %param.17) | data formatting | bytes 32768 | tf_op args[4]
  1.5 0.0 copy-done.4
  1.5 0.0 copy-start
  1.5 0.9 %copy-done = bf16[256,256]{1,0:T(8,128)(2,1)S(1)} copy-done((bf16[256,256]{1,0:T(8,128)(2,1)S(1)}, bf16[256,256]{1,0:T(8,128)(2,1)}, u32[]{:S(2)}) %copy-start) | copy-done | bytes 131096
  2.4 0.0 copy-start.1
  2.4 0.9 %copy-done.1 = bf16[256,256]{1,0:T(8,128)(2,1)S(1)} copy-done((bf16[256,256]{1,0:T(8,128)(2,1)S(1)}, bf16[256,256]{1,0:T(8,128)(2,1)}, u32[]{:S(2)}) %copy-start.1) | copy-done | bytes 131096
  3.3 0.0 copy-start.2
  3.3 0.9 %copy-done.2 = bf16[256,256]{1,0:T(8,128)(2,1)S(1)} copy-done((bf16[256,256]{1,0:T(8,128)(2,1)S(1)}, bf16[256,256]{1,0:T(8,128)(2,1)}, u32[]{:S(2)}) %copy-start.2) | copy-done | bytes 131096
  4.2 0.0 copy-start.3
  4.2 0.9 %copy-done.3 = bf16[256,256]{1,0:T(8,128)(2,1)S(1)} copy-done((bf16[256,256]{1,0:T(8,128)(2,1)S(1)}, bf16[256,256]{1,0:T(8,128)(2,1)}, u32[]{:S(2)}) %copy-start.3) | copy-done | bytes 131096
  5.1 0.0 copy-start.5
  5.1 0.8 %copy-done.5 = f32[1,16384]{1,0:T(1,128)S(1)} copy-done((f32[1,16384]{1,0:T(1,128)S(1)}, f32[1,16384]{1,0:T(1,128)}, u32[]{:S(2)}) %copy-start.5) | copy-done | bytes 65560
  6.0 0.0 copy-start.6
  6.0 0.8 %copy-done.6 = f32[128,128]{1,0:T(8,128)S(1)} copy-done((f32[128,128]{1,0:T(8,128)S(1)}, f32[128,128]{1,0:T(8,128)}, u32[]{:S(2)}) %copy-start.6) | copy-done | bytes 65560
  6.8 0.0 copy-start.7
  6.8 0.8 %copy-done.7 = f32[128,128]{1,0:T(8,128)S(1)} copy-done((f32[128,128]{1,0:T(8,128)S(1)}, f32[128,128]{1,0:T(8,128)}, u32[]{:S(2)}) %copy-start.7) | copy-done | bytes 65560
  7.6 0.0 copy-start.8
  7.6 0.8 %copy-done.8 = f32[128,128]{1,0:T(8,128)S(1)} copy-done((f32[128,128]{1,0:T(8,128)S(1)}, f32[128,128]{1,0:T(8,128)}, u32[]{:S(2)}) %copy-start.8) | copy-done | bytes 65560
  8.5 0.0 copy-start.9
  8.5 0.8 %copy-done.9 = f32[128,128]{1,0:T(8,128)S(1)} copy-done((f32[128,128]{1,0:T(8,128)S(1)}, f32[128,128]{1,0:T(8,128)}, u32[]{:S(2)}) %copy-start.9) | copy-done | bytes 65560
  9.3 0.0 copy-start.10
  9.3 0.8 %copy-done.10 = f32[128,128]{1,0:T(8,128)S(1)} copy-done((f32[128,128]{1,0:T(8,128)S(1)}, f32[128,128]{1,0:T(8,128)}, u32[]{:S(2)}) %copy-start.10) | copy-done | bytes 65560
  10.2 0.0 copy-start.11
  10.2 0.8 %copy-done.11 = f32[128,128]{1,0:T(8,128)S(1)} copy-done((f32[128,128]{1,0:T(8,128)S(1)}, f32[128,128]{1,0:T(8,128)}, u32[]{:S(2)}) %copy-start.11) | copy-done | bytes 65560
  11.0 53.1 %adjoint_step.1 = (f32[128,128]{1,0:T(8,128)S(1)}, f32[128,32]{1,0:T(8,128)S(1)}) custom-call(s32[128,128]{1,0:T(8,128)S(1)} %bitcast.3, f32[128,128]{1,0:T(8,128)S(1)} %bitcast.4, f32[128,128]{1,0:T(8,128)S(1)} %copy-done.6, f32[128,128]{1,0:T(8,128)S(1)} %copy-done.7, f32[128,32]{1,0:T(8,128)S(1)} %copy.15.refs_4_, bf16[256,256]{1,0:T(8,128)(2,1)S(1)} %copy-done.3, ...), custom_call_target="tpu_custom_call" | custom-call | tf_op jit(solution)/shard_map/adjoint_step/pallas_call | solution.py:267
  64.1 0.7 %copy.16 = f32[128,32]{0,1:T(8,128)} copy(f32[128,32]{1,0:T(8,128)S(1)} %get-tuple-element.7) | data formatting | bytes 32768
  64.8 0.6 copy.18
Async XLA Ops:
  0.6 0.9 %copy-start.4 = (s32[1,1,16384]{2,1,0:T(1,128)S(1)}, s32[1,1,16384]{2,1,0:T(1,128)}, u32[]{:S(2)}) copy-start(s32[1,1,16384]{2,1,0:T(1,128)} %param.13) | copy-start | bytes 196612
  1.5 0.9 %copy-start = (bf16[256,256]{1,0:T(8,128)(2,1)S(1)}, bf16[256,256]{1,0:T(8,128)(2,1)}, u32[]{:S(2)}) copy-start(bf16[256,256]{1,0:T(8,128)(2,1)} %constant.19.clone.refs_8_) | copy-start | bytes 393220
  2.4 0.9 %copy-start.1 = (bf16[256,256]{1,0:T(8,128)(2,1)S(1)}, bf16[256,256]{1,0:T(8,128)(2,1)}, u32[]{:S(2)}) copy-start(bf16[256,256]{1,0:T(8,128)(2,1)} %constant.18.clone.refs_7_) | copy-start | bytes 393220
  3.3 0.9 %copy-start.2 = (bf16[256,256]{1,0:T(8,128)(2,1)S(1)}, bf16[256,256]{1,0:T(8,128)(2,1)}, u32[]{:S(2)}) copy-start(bf16[256,256]{1,0:T(8,128)(2,1)} %constant.17.clone.refs_6_) | copy-start | bytes 393220
  4.2 0.9 %copy-start.3 = (bf16[256,256]{1,0:T(8,128)(2,1)S(1)}, bf16[256,256]{1,0:T(8,128)(2,1)}, u32[]{:S(2)}) copy-start(bf16[256,256]{1,0:T(8,128)(2,1)} %constant.16.clone.refs_5_) | copy-start | bytes 393220
  5.1 0.8 %copy-start.5 = (f32[1,16384]{1,0:T(1,128)S(1)}, f32[1,16384]{1,0:T(1,128)}, u32[]{:S(2)}) copy-start(f32[1,16384]{1,0:T(1,128)} %param.14) | copy-start | bytes 196612
  6.0 0.8 %copy-start.6 = (f32[128,128]{1,0:T(8,128)S(1)}, f32[128,128]{1,0:T(8,128)}, u32[]{:S(2)}) copy-start(f32[128,128]{1,0:T(8,128)} %refs_2_.1) | copy-start | bytes 196612
  6.8 0.8 %copy-start.7 = (f32[128,128]{1,0:T(8,128)S(1)}, f32[128,128]{1,0:T(8,128)}, u32[]{:S(2)}) copy-start(f32[128,128]{1,0:T(8,128)} %refs_3_.1) | copy-start | bytes 196612
  7.6 0.8 %copy-start.8 = (f32[128,128]{1,0:T(8,128)S(1)}, f32[128,128]{1,0:T(8,128)}, u32[]{:S(2)}) copy-start(f32[128,128]{1,0:T(8,128)} %constant.23.clone.refs_12_) | copy-start | bytes 196612
  8.5 0.8 %copy-start.9 = (f32[128,128]{1,0:T(8,128)S(1)}, f32[128,128]{1,0:T(8,128)}, u32[]{:S(2)}) copy-start(f32[128,128]{1,0:T(8,128)} %constant.22.clone.refs_11_) | copy-start | bytes 196612
  9.3 0.8 %copy-start.10 = (f32[128,128]{1,0:T(8,128)S(1)}, f32[128,128]{1,0:T(8,128)}, u32[]{:S(2)}) copy-start(f32[128,128]{1,0:T(8,128)} %constant.21.clone.refs_10_) | copy-start | bytes 196612
  10.2 0.8 %copy-start.11 = (f32[128,128]{1,0:T(8,128)S(1)}, f32[128,128]{1,0:T(8,128)}, u32[]{:S(2)}) copy-start(f32[128,128]{1,0:T(8,128)} %constant.20.clone.refs_9_) | copy-start | bytes 196612

commit v2 on v1

v2 whole, which is shorter than its diff:
```python
import math

import jax
import jax.numpy as jnp
import numpy as np
from jax import lax
from jax.experimental import pallas as pl
from jax.experimental.pallas import tpu as pltpu
from jax.sharding import PartitionSpec as P

MESH = pl.DeviceIdType.MESH
n = 128
f32 = jnp.float32
bf16 = jnp.bfloat16


def split_np(table):
    table = table.astype(np.float32)
    high = table.astype(jnp.bfloat16)
    low = (table - high.astype(np.float32)).astype(jnp.bfloat16)
    return high, low


def tables(samples):
    index = np.arange(n)
    product = index[:, None] * index[None, :]
    angle = 2.0 * math.pi * (product % n) / n
    cosine, sine = np.cos(angle), np.sin(angle)
    forward = np.block([[cosine, sine], [-sine, cosine]])
    inverse = np.block([[cosine, -sine], [sine, cosine]])
    turn = 2.0 * math.pi * product / (n * n)
    far = 2.0 * math.pi * product / samples
    f_high, f_low = split_np(forward)
    i_high, i_low = split_np(inverse)
    rest = [np.cos(turn), -np.sin(turn), np.cos(far), -np.sin(far)]
    dft = np.stack([i_high, i_low, f_high, f_low])
    return dft, np.stack(rest).astype(np.float32)


def split(x):
    high = x.astype(bf16)
    low = (x - high.astype(f32)).astype(bf16)
    return high, low


def mm(a, b):
    return jnp.dot(a, b, preferred_element_type=f32)


def table_left(t_high, t_low, data):
    high, low = split(data)
    return mm(t_high, high) + (mm(t_high, low) + mm(t_low, high))


def table_right(data, t_high, t_low):
    high, low = split(data)
    return mm(high, t_high) + (mm(low, t_high) + mm(high, t_low))


far_first = (4, 3, 5, 2, 6, 1, 7, 0)


def kernel(
    probes,
    bits_hbm,
    noise_hbm,
    kernel_hbm,
    symbol_hbm,
    prev_hbm,
    dft_hbm,
    turn_hbm,
    resid_ref,
    grad_ref,
    bits_ref,
    noise_ref,
    kernel_ref,
    symbol_ref,
    prev_ref,
    dft_ref,
    turn_ref,
    out1,
    in1,
    out2,
    in2,
    out3,
    in3,
    out4,
    in4,
    out5,
    in5,
    line1,
    near1,
    line2,
    near2,
    load,
    send,
    recv,
):
    me = lax.axis_index("seq")
    mine = lax.axis_index("probe")
    samples = n * n * n
    ring, plane = me // 16, lax.rem(me, 16)
    across, core = plane // 2, lax.rem(plane, 2)

    loads = [
        pltpu.make_async_copy(source, target, load.at[place])
        for place, (source, target) in enumerate(
            (
                (bits_hbm, bits_ref),
                (dft_hbm, dft_ref),
                (turn_hbm, turn_ref),
                (noise_hbm, noise_ref),
                (symbol_hbm, symbol_ref),
                (kernel_hbm, kernel_ref),
                (prev_hbm, prev_ref),
            )
        )
    ]
    for copy in loads:
        copy.start()

    inner = []
    for shift in far_first:
        spot = lax.rem(across + shift, 8) * 2
        inner += [spot + (1 - core), spot + core]

    def each_peer(act):
        @pl.loop(0, 7)
        def _(turn):
            shift = 4 + ((turn + 1) // 2) * (1 - 2 * lax.rem(turn, 2))
            start = lax.rem(ring + shift, 8) * 16
            for spot in inner:
                act(start + spot)

        for spot in inner[:-1]:
            act(ring * 16 + spot)

    barrier = pltpu.get_barrier_semaphore()

    def greet(peer):
        pl.semaphore_signal(barrier, inc=1, device_id={"seq": peer}, device_id_type=MESH)

    each_peer(greet)
    for i in range(1, probes):
        other = lax.rem(mine + i, probes)
        pl.semaphore_signal(barrier, inc=1, device_id={"probe": other}, device_id_type=MESH)

    def exchange(source, target, slot, rows):
        landing = target.at[pl.ds(me * rows, rows)]

        def put(peer):
            pltpu.make_async_remote_copy(
                src_ref=source.at[pl.ds(peer * rows, rows)],
                dst_ref=landing,
                send_sem=send.at[slot],
                recv_sem=recv.at[slot],
                device_id={"seq": peer},
                device_id_type=MESH,
            ).start()

        each_peer(put)
        own = source.at[pl.ds(me * rows, rows)]
        pltpu.make_async_copy(own, landing, recv.at[slot]).start()

    def arrived(target, slot):
        pltpu.make_async_copy(target, target, recv.at[slot]).wait()

    def sent(source, slot, rows):
        part = source.at[pl.ds(0, rows)]
        pltpu.make_async_copy(part, part, send.at[slot]).wait()

    def row(place, count):
        return pl.ds(place, n, stride=count)

    loads[0].wait()
    sign = (2 * bits_ref[...] - 1).astype(f32).T
    loads[1].wait()
    loads[2].wait()
    ih, il, fh, fl = [dft_ref.at[place] for place in range(4)]
    turn_c, turn_s = turn_ref[0], turn_ref[1]
    row_c = jnp.broadcast_to(turn_ref[2, pl.ds(me, 1), :], (n, n))
    row_s = jnp.broadcast_to(turn_ref[3, pl.ds(me, 1), :], (n, n))
    col_c = jnp.broadcast_to(turn_ref[0, pl.ds(me, 1), :], (n, n)).T
    col_s = jnp.broadcast_to(turn_ref[1, pl.ds(me, 1), :], (n, n)).T
    glob_c = col_c * row_c - col_s * row_s
    glob_s = col_c * row_s + col_s * row_c

    def forward(field, exact=False):
        right_h, right_l = ih[0:n, :], il[0:n, :]
        if exact:
            high = field.astype(bf16)
            part = mm(high, right_h) + mm(high, right_l)
        else:
            part = table_right(field, right_h, right_l)
        real, imag = part[:, 0:n], part[:, n:]
        data = jnp.concatenate(
            [real * turn_c - imag * turn_s, real * turn_s + imag * turn_c], axis=0
        )
        full = table_left(fh[...], fl[...], data)
        real, imag = full[0:n], full[n:]
        return real * glob_c - imag * glob_s, real * glob_s + imag * glob_c

    def columns(target, place, count):
        data = jnp.concatenate(
            [target[row(place, count), :], target[row(place + 1, count), :]], axis=0
        )
        full = table_left(fh[...], fl[...], data)
        return full[0:n], full[n:]

    base = forward(sign, exact=True)
    out1[row(0, 2), :] = base[0]
    out1[row(1, 2), :] = base[1]
    pl.semaphore_wait(barrier, n - 1 + probes - 1)
    exchange(out1, in1, 0, 2)
    loads[3].wait()
    noise = noise_ref[...].T
    noisy = forward(noise * sign)
    out2[row(0, 2), :] = noisy[0]
    out2[row(1, 2), :] = noisy[1]
    exchange(out2, in2, 1, 2)
    loads[4].wait()
    inv = 1.0 / symbol_ref[...].T
    loads[5].wait()
    eig = kernel_ref[...].T
    loads[6].wait()

    arrived(in1, 0)
    s_real, s_imag = columns(in1, 0, 2)
    scaled_real, scaled_imag = s_real * inv, s_imag * inv
    pair_real = scaled_real - eig * scaled_imag
    pair_imag = scaled_imag + eig * scaled_real
    back = table_left(ih[...], il[...], jnp.concatenate([pair_real, pair_imag], axis=0))
    out3[row(0, 2), :] = back[0:n]
    out3[row(1, 2), :] = back[n:]
    exchange(out3, in3, 2, 2)
    power = s_real * s_real + s_imag * s_imag
    arrived(in2, 1)
    t_real, t_imag = columns(in2, 0, 2)
    t_dot = t_real * s_real + t_imag * s_imag

    arrived(in3, 2)
    real, imag = in3[row(0, 2), :], in3[row(1, 2), :]
    data = jnp.concatenate(
        [real * glob_c + imag * glob_s, imag * glob_c - real * glob_s], axis=0
    )
    full = table_left(ih[...], il[...], data)
    real, imag = full[0:n], full[n:]
    data = jnp.concatenate(
        [real * turn_c + imag * turn_s, imag * turn_c - real * turn_s], axis=1
    )
    spatial = table_right(data, fh[...], fl[...]) * (1.0 / samples)
    precond, circulant = spatial[:, 0:n], spatial[:, n:]
    damped = noise * precond
    image = circulant + damped
    first = forward(damped)
    second = forward(noise * image)
    for place, value in enumerate(first + second):
        out4[row(place, 4), :] = value
    parts = (sign * precond, precond * image, sign * image, image * image)
    line1[...] = jnp.concatenate([jnp.sum(part, axis=0, keepdims=True) for part in parts], axis=0)

    for i in range(1, 16):
        spot = lax.rem(plane + i, 16)
        pltpu.make_async_remote_copy(
            src_ref=line1,
            dst_ref=near1.at[plane],
            send_sem=send.at[5],
            recv_sem=recv.at[5],
            device_id={"seq": ring * 16 + spot},
            device_id_type=MESH,
        ).start()
    pltpu.make_async_copy(line1, near1.at[plane], recv.at[5]).start()
    exchange(out4, in4, 3, 4)
    arrived(near1, 5)
    lines = near1[0]
    for place in range(1, 16):
        lines = lines + near1[place]
    line2[...] = lines
    for i in range(1, 8):
        spot = lax.rem(ring + i, 8)
        pltpu.make_async_remote_copy(
            src_ref=line2,
            dst_ref=near2.at[ring],
            send_sem=send.at[6],
            recv_sem=recv.at[6],
            device_id={"seq": spot * 16 + plane},
            device_id_type=MESH,
        ).start()
    pltpu.make_async_copy(line2, near2.at[ring], recv.at[6]).start()
    sent(out1, 0, 2 * (n - 1))
    sent(out2, 1, 2 * (n - 1))
    sent(out3, 2, 2 * (n - 1))
    part = near1.at[pl.ds(0, 15)]
    pltpu.make_async_copy(part, part, send.at[5]).wait()
    arrived(near2, 6)
    lines = near2[0]
    for place in range(1, 8):
        lines = lines + near2[place]
    sums = jnp.sum(lines, axis=1, keepdims=True)
    numerator, curvature, straight, squared = [sums[place : place + 1] for place in range(4)]
    step = numerator / curvature
    weight = -2.0 * (straight - step * squared)
    over = weight / curvature
    double = 2.0 * over * step
    resid_ref[...] = (sign - step * image).T
    part = near2.at[pl.ds(0, 7)]
    pltpu.make_async_copy(part, part, send.at[6]).wait()
    base_dot = over * power - (2.0 * step) * (eig * power + t_dot)
    slope = (2.0 * step * step) * eig - double
    fixed = base_dot + slope * (eig * inv * power)
    scale = (inv * inv) * (-1.0 / (samples * probes))

    arrived(in4, 3)
    y_real, y_imag = columns(in4, 0, 4)
    y_dot = y_real * s_real + y_imag * s_imag
    q_real, q_imag = columns(in4, 2, 4)
    q_dot = q_real * s_real + q_imag * s_imag
    share = (fixed + slope * y_dot + (2.0 * step * step) * q_dot) * scale
    width = n // probes
    for place in range(probes):
        out5[place] = share[place * width : (place + 1) * width]

    for i in range(1, probes):
        other = lax.rem(mine + i, probes)
        pltpu.make_async_remote_copy(
            src_ref=out5.at[other],
            dst_ref=in5.at[mine],
            send_sem=send.at[4],
            recv_sem=recv.at[4],
            device_id={"probe": other},
            device_id_type=MESH,
        ).start()
    pltpu.make_async_copy(out5.at[mine], in5.at[mine], recv.at[4]).start()
    sent(out4, 3, 4 * (n - 1))
    arrived(in5, 4)
    own = in5[0]
    for place in range(1, probes):
        own = own + in5[place]
    grad_ref[...] = prev_ref[...] + own
    rest = out5.at[pl.ds(0, probes - 1)]
    pltpu.make_async_copy(rest, rest, send.at[4]).wait()


def shards(probes, probe_bits, noise_var, kernel_spectrum, symbol, grad_prev):
    width = grad_prev.shape[1]
    vmem = pl.BlockSpec(memory_space=pltpu.VMEM)
    dft, turn = tables(n * n * n)
    block = pltpu.VMEM((n, n), f32)
    pair = pltpu.VMEM((2 * n, n), f32)
    quad = pltpu.VMEM((4 * n, n), f32)
    quarter = pltpu.VMEM((probes, width, n), f32)
    line = pltpu.VMEM((4, n), f32)
    semaphores = pltpu.SemaphoreType.DMA((7,))
    resid, grad = pl.pallas_call(
        lambda *refs: kernel(probes, *refs),
        out_shape=(
            jax.ShapeDtypeStruct((n, n), f32),
            jax.ShapeDtypeStruct((width, n), f32),
        ),
        in_specs=[pl.BlockSpec(memory_space=pl.ANY)] * 7,
        out_specs=(vmem, vmem),
        scratch_shapes=[
            pltpu.VMEM((n, n), jnp.int32),
            block,
            block,
            block,
            pltpu.VMEM((width, n), f32),
            pltpu.VMEM(dft.shape, bf16),
            pltpu.VMEM(turn.shape, f32),
        ]
        + [pair] * 6
        + [quad, quad, quarter, quarter]
        + [line, pltpu.VMEM((16, 4, n), f32), line, pltpu.VMEM((8, 4, n), f32)]
        + [semaphores] * 3,
        compiler_params=pltpu.CompilerParams(
            collective_id=0, has_side_effects=True, vmem_limit_bytes=66_000_000
        ),
        name="adjoint_step",
    )(
        probe_bits.reshape(n, n),
        noise_var.reshape(n, n),
        kernel_spectrum,
        symbol,
        grad_prev.T,
        jnp.asarray(dft),
        jnp.asarray(turn),
    )
    return resid.reshape(probe_bits.shape), grad.T


def solution(mesh):
    placed = (
        P("probe", "seq", None),
        P("seq", None),
        P("seq", None),
        P("seq", None),
        P("seq", "probe"),
    )
    probes = mesh.shape["probe"]
    return jax.shard_map(
        lambda *args: shards(probes, *args),
        mesh=mesh,
        in_specs=placed,
        out_specs=(P("probe", "seq", None), P("seq", "probe")),
        check_vma=False,
    )
```

time: 66 us -> 52.1 us (0.79)
  local copies, waits for them, and re-layouts: 11.6 us -> 2.09 us
  Pallas kernels: 53.1 us -> 49.2 us
    unnamed x27 -> x4, local copies, waits for them, and re-layouts: 11.6 us -> 2.09 us
    pallas_call x1, Pallas kernels: 53.1 us -> 49.2 us  [shards(): pl.pallas_call(lambda *refs: kernel(probes, *refs), out_shape=(jax.ShapeD...]
where the time goes in v2:
time: 52.1 us; the launch traced here: 51.9 us
  Pallas kernels  49.2 us (94%)
  local copies, waits for them, and re-layouts  2.09 us (4%)
  between operations  0.65 us (1%)
    pallas_call x1, Pallas kernels, shards(): pl.pallas_call(lambda *refs: kernel(probes, *refs), out_shape=(jax.ShapeD...  49.2 us
    unnamed x4, local copies, waits for them, and re-layouts  2.09 us

profile of v2, /device:TPU:1, one launch (start us, length us, event | category | flops | bytes accessed | tf_op | source)
XLA Modules:
  0.0 51.9 jit_solution(2709813162893326643)
XLA Ops:
  0.6 49.2 %adjoint_step.1 = (f32[128,128]{1,0:T(8,128)}, f32[32,128]{1,0:T(8,128)}) custom-call(s32[128,128]{1,0:T(8,128)} %bitcast.5, f32[128,128]{1,0:T(8,128)} %bitcast.6, f32[128,128]{1,0:T(8,128)} %refs_2_.1, f32[128,128]{1,0:T(8,128)} %refs_3_.1, f32[32,128]{1,0:T(8,128)} %bitcast.8, bf16[4,256,256]{2,1,0:T(8,128)(2,1)} %constant.4.clone.refs_5_, ...), custom_call_target="tpu_custom_call" | custom-call | tf_op jit(solution)/shard_map/adjoint_step/pallas_call | solution.py:354
  49.8 0.0 copy-start
  49.8 1.5 %copy.11 = f32[1,1,16384]{2,1,0:T(1,128)} copy(f32[1,1,16384]{2,1,0:T(1,128)} %bitcast.7) | data formatting | bytes 131072
  51.3 0.0 copy-done
  51.3 0.6 %copy.12 = f32[128,32]{0,1:T(8,128)} copy(f32[128,32]{0,1:T(8,128)S(1)} %bitcast.9) | data formatting | bytes 32768
Async XLA Ops:
  49.8 1.5 %copy-start = (f32[32,128]{1,0:T(8,128)S(1)}, f32[32,128]{1,0:T(8,128)}, u32[]{:S(2)}) copy-start(f32[32,128]{1,0:T(8,128)} %get-tuple-element.5) | copy-start | bytes 49156

commit v3 on v2

--- a/solution.py
+++ b/solution.py
@@ -49,15 +49,41 @@
 
 def table_left(t_high, t_low, data):
     high, low = split(data)
-    return mm(t_high, high) + (mm(t_high, low) + mm(t_low, high))
+    return mm(
+        jnp.concatenate([t_high, t_high, t_low], axis=1),
+        jnp.concatenate([high, low, high], axis=0),
+    )
 
 
 def table_right(data, t_high, t_low):
     high, low = split(data)
-    return mm(high, t_high) + (mm(low, t_high) + mm(high, t_low))
-
-
-far_first = (4, 3, 5, 2, 6, 1, 7, 0)
+    return mm(
+        jnp.concatenate([high, low, high], axis=1),
+        jnp.concatenate([t_high, t_high, t_low], axis=0),
+    )
+
+
+def far_first():
+    def hops(shift):
+        return min(shift, 8 - shift)
+
+    def side(shift):
+        return 0 if shift in (0, 4) else (1 if shift < 4 else -1)
+
+    order = []
+    for distance in range(8, -1, -1):
+        groups = {}
+        for first in range(8):
+            for second in range(8):
+                if hops(first) + hops(second) == distance:
+                    key = (side(first), side(second))
+                    groups.setdefault(key, []).append((first, second))
+        keys = sorted(groups, key=lambda key: (key[0] * key[1], key))
+        while any(groups.values()):
+            for key in keys:
+                if groups[key]:
+                    order.append(groups[key].pop())
+    return order
 
 
 def kernel(
@@ -119,21 +145,14 @@
     for copy in loads:
         copy.start()
 
-    inner = []
-    for shift in far_first:
-        spot = lax.rem(across + shift, 8) * 2
-        inner += [spot + (1 - core), spot + core]
+    rings = [lax.rem(ring + shift, 8) * 16 for shift in range(8)]
+    spots = [lax.rem(across + shift, 8) * 2 for shift in range(8)]
 
     def each_peer(act):
-        @pl.loop(0, 7)
-        def _(turn):
-            shift = 4 + ((turn + 1) // 2) * (1 - 2 * lax.rem(turn, 2))
-            start = lax.rem(ring + shift, 8) * 16
-            for spot in inner:
-                act(start + spot)
-
-        for spot in inner[:-1]:
-            act(ring * 16 + spot)
+        for first, second in far_first():
+            act(rings[first] + (spots[second] + (1 - core)))
+            if (first, second) != (0, 0):
+                act(rings[first] + (spots[second] + core))
 
     barrier = pltpu.get_barrier_semaphore()
 
@@ -189,7 +208,10 @@
         right_h, right_l = ih[0:n, :], il[0:n, :]
         if exact:
             high = field.astype(bf16)
-            part = mm(high, right_h) + mm(high, right_l)
+            part = mm(
+                jnp.concatenate([high, high], axis=1),
+                jnp.concatenate([right_h, right_l], axis=0),
+            )
         else:
             part = table_right(field, right_h, right_l)
         real, imag = part[:, 0:n], part[:, n:]
@@ -320,7 +342,7 @@
     for place in range(probes):
         out5[place] = share[place * width : (place + 1) * width]
 
-    for i in range(1, probes):
+    for i in sorted(range(1, probes), key=lambda i: -min(i, probes - i)):
         other = lax.rem(mine + i, probes)
         pltpu.make_async_remote_copy(
             src_ref=out5.at[other],
@@ -351,6 +373,15 @@
     quarter = pltpu.VMEM((probes, width, n), f32)
     line = pltpu.VMEM((4, n), f32)
     semaphores = pltpu.SemaphoreType.DMA((7,))
+    held = [
+        probe_bits.reshape(n, n),
+        noise_var.reshape(n, n),
+        kernel_spectrum,
+        symbol,
+        grad_prev.T,
+        jnp.asarray(dft),
+        jnp.asarray(turn),
+    ]
     resid, grad = pl.pallas_call(
         lambda *refs: kernel(probes, *refs),
         out_shape=(
@@ -373,18 +404,10 @@
         + [line, pltpu.VMEM((16, 4, n), f32), line, pltpu.VMEM((8, 4, n), f32)]
         + [semaphores] * 3,
         compiler_params=pltpu.CompilerParams(
-            collective_id=0, has_side_effects=True, vmem_limit_bytes=66_000_000
+            collective_id=0, has_side_effects=True, vmem_limit_bytes=24_000_000
         ),
         name="adjoint_step",
-    )(
-        probe_bits.reshape(n, n),
-        noise_var.reshape(n, n),
-        kernel_spectrum,
-        symbol,
-        grad_prev.T,
-        jnp.asarray(dft),
-        jnp.asarray(turn),
-    )
+    )(*[pltpu.with_memory_space_constraint(part, pltpu.MemorySpace.HBM) for part in held])
     return resid.reshape(probe_bits.shape), grad.T
 
 

time: 52.1 us -> 53 us (1.017)
  Pallas kernels: 49.2 us -> 51 us
  local copies, waits for them, and re-layouts: 2.09 us -> 1.24 us
    pallas_call x1, Pallas kernels: 49.2 us -> 51 us  [shards(): pl.pallas_call(lambda *refs: kernel(probes, *refs), out_shape=(jax.ShapeD...]
    unnamed x4 -> x2, local copies, waits for them, and re-layouts: 2.09 us -> 1.24 us
where the time goes in v3:
time: 53 us; the launch traced here: 52.8 us
  Pallas kernels  51 us (96%)
  local copies, waits for them, and re-layouts  1.24 us (2%)
  between operations  0.64 us (1%)
    pallas_call x1, Pallas kernels, shards(): pl.pallas_call(lambda *refs: kernel(probes, *refs), out_shape=(jax.ShapeD...  51 us
    unnamed x2, local copies, waits for them, and re-layouts  1.24 us

profile of v3, /device:TPU:1, one launch (start us, length us, event | category | flops | bytes accessed | tf_op | source)
XLA Modules:
  0.0 52.8 jit_solution(4915964245124203104)
XLA Ops:
  0.6 51.0 %adjoint_step.1 = (f32[128,128]{1,0:T(8,128)S(1)}, f32[32,128]{1,0:T(8,128)S(1)}) custom-call(s32[128,128]{1,0:T(8,128)} %bitcast.7, f32[128,128]{1,0:T(8,128)} %bitcast.8, f32[128,128]{1,0:T(8,128)} %refs_2_.1, f32[128,128]{1,0:T(8,128)} %refs_3_.1, f32[32,128]{1,0:T(8,128)} %bitcast.9, bf16[4,256,256]{2,1,0:T(8,128)(2,1)} %constant.4.clone.refs_5_, ...), custom_call_target="tpu_custom_call" | custom-call | tf_op jit(solution)/shard_map/adjoint_step/pallas_call | solution.py:385
  51.6 0.6 %copy.11 = f32[1,1,16384]{2,1,0:T(1,128)} copy(f32[1,1,16384]{2,1,0:T(1,128)S(1)} %bitcast.5) | data formatting | bytes 131072
  52.2 0.6 %copy.12 = f32[128,32]{0,1:T(8,128)} copy(f32[128,32]{0,1:T(8,128)S(1)} %bitcast.6) | data formatting | bytes 32768

commit v4 on v2

--- a/solution.py
+++ b/solution.py
@@ -49,12 +49,18 @@
 
 def table_left(t_high, t_low, data):
     high, low = split(data)
-    return mm(t_high, high) + (mm(t_high, low) + mm(t_low, high))
+    return mm(
+        jnp.concatenate([t_high, t_high, t_low], axis=1),
+        jnp.concatenate([high, low, high], axis=0),
+    )
 
 
 def table_right(data, t_high, t_low):
     high, low = split(data)
-    return mm(high, t_high) + (mm(low, t_high) + mm(high, t_low))
+    return mm(
+        jnp.concatenate([high, low, high], axis=1),
+        jnp.concatenate([t_high, t_high, t_low], axis=0),
+    )
 
 
 far_first = (4, 3, 5, 2, 6, 1, 7, 0)
@@ -116,9 +122,6 @@
             )
         )
     ]
-    for copy in loads:
-        copy.start()
-
     inner = []
     for shift in far_first:
         spot = lax.rem(across + shift, 8) * 2
@@ -144,6 +147,9 @@
     for i in range(1, probes):
         other = lax.rem(mine + i, probes)
         pl.semaphore_signal(barrier, inc=1, device_id={"probe": other}, device_id_type=MESH)
+
+    for copy in loads:
+        copy.start()
 
     def exchange(source, target, slot, rows):
         landing = target.at[pl.ds(me * rows, rows)]
@@ -320,7 +326,7 @@
     for place in range(probes):
         out5[place] = share[place * width : (place + 1) * width]
 
-    for i in range(1, probes):
+    for i in sorted(range(1, probes), key=lambda i: -min(i, probes - i)):
         other = lax.rem(mine + i, probes)
         pltpu.make_async_remote_copy(
             src_ref=out5.at[other],
@@ -351,6 +357,15 @@
     quarter = pltpu.VMEM((probes, width, n), f32)
     line = pltpu.VMEM((4, n), f32)
     semaphores = pltpu.SemaphoreType.DMA((7,))
+    held = [
+        probe_bits.reshape(n, n),
+        noise_var.reshape(n, n),
+        kernel_spectrum,
+        symbol,
+        grad_prev.T,
+        jnp.asarray(dft),
+        jnp.asarray(turn),
+    ]
     resid, grad = pl.pallas_call(
         lambda *refs: kernel(probes, *refs),
         out_shape=(
@@ -373,18 +388,10 @@
         + [line, pltpu.VMEM((16, 4, n), f32), line, pltpu.VMEM((8, 4, n), f32)]
         + [semaphores] * 3,
         compiler_params=pltpu.CompilerParams(
-            collective_id=0, has_side_effects=True, vmem_limit_bytes=66_000_000
+            collective_id=0, has_side_effects=True, vmem_limit_bytes=24_000_000
         ),
         name="adjoint_step",
-    )(
-        probe_bits.reshape(n, n),
-        noise_var.reshape(n, n),
-        kernel_spectrum,
-        symbol,
-        grad_prev.T,
-        jnp.asarray(dft),
-        jnp.asarray(turn),
-    )
+    )(*[pltpu.with_memory_space_constraint(part, pltpu.MemorySpace.HBM) for part in held])
     return resid.reshape(probe_bits.shape), grad.T
 
 

time: 52.1 us -> 50 us (0.960)
  Pallas kernels: 49.2 us -> 48 us
  local copies, waits for them, and re-layouts: 2.09 us -> 1.24 us
    pallas_call x1, Pallas kernels: 49.2 us -> 48 us  [shards(): pl.pallas_call(lambda *refs: kernel(probes, *refs), out_shape=(jax.ShapeD...]
    unnamed x4 -> x2, local copies, waits for them, and re-layouts: 2.09 us -> 1.24 us
where the time goes in v4:
time: 50 us; the launch traced here: 49.9 us
  Pallas kernels  48 us (96%)
  local copies, waits for them, and re-layouts  1.24 us (2%)
  between operations  0.64 us (1%)
    pallas_call x1, Pallas kernels, shards(): pl.pallas_call(lambda *refs: kernel(probes, *refs), out_shape=(jax.ShapeD...  48 us
    unnamed x2, local copies, waits for them, and re-layouts  1.24 us

profile of v4, /device:TPU:1, one launch (start us, length us, event | category | flops | bytes accessed | tf_op | source)
XLA Modules:
  0.0 49.9 jit_solution(10042810785020433855)
XLA Ops:
  0.6 48.0 %adjoint_step.1 = (f32[128,128]{1,0:T(8,128)S(1)}, f32[32,128]{1,0:T(8,128)S(1)}) custom-call(s32[128,128]{1,0:T(8,128)} %bitcast.7, f32[128,128]{1,0:T(8,128)} %bitcast.8, f32[128,128]{1,0:T(8,128)} %refs_2_.1, f32[128,128]{1,0:T(8,128)} %refs_3_.1, f32[32,128]{1,0:T(8,128)} %bitcast.9, bf16[4,256,256]{2,1,0:T(8,128)(2,1)} %constant.4.clone.refs_5_, ...), custom_call_target="tpu_custom_call" | custom-call | tf_op jit(solution)/shard_map/adjoint_step/pallas_call | solution.py:369
  48.7 0.6 %copy.11 = f32[1,1,16384]{2,1,0:T(1,128)} copy(f32[1,1,16384]{2,1,0:T(1,128)S(1)} %bitcast.5) | data formatting | bytes 131072
  49.3 0.6 %copy.12 = f32[128,32]{0,1:T(8,128)} copy(f32[128,32]{0,1:T(8,128)S(1)} %bitcast.6) | data formatting | bytes 32768
